TPU v7x, 32 devices: a whole 2x2x4 slice. The times are simulated.
32 devices in a mesh: kvp: 16 (over z, y, x), tp: 2 (over core).
Axes of the slice: x: 2, y: 2, z: 4, core: 2. Of those that a mesh axis runs over, the one named last changes fastest.
Arguments:
- queries: bfloat16 [8, 8192], P(None, 'tp'), may hold values from -12 to 12
- key_pool: bfloat16 [512, 64, 1024], P('kvp', None, 'tp'), may hold values from -5 to 5
- value_pool: bfloat16 [512, 64, 1024], P('kvp', None, 'tp'), may hold values from -5 to 5
- block_table: int32 [16, 32], P('kvp'), may hold values from 0 to 31, each once within a row
- lengths: int32 [8], replicated, may hold values from 1 to 4096, 20480 in all
- residual_in: float32 [8, 8192], P(None, 'kvp'), may hold values from -12 to 12
- out_weight: bfloat16 [8192, 8192], P('tp', 'kvp'), may hold values from -0.0625 to 0.0625
- norm_gain: bfloat16 [8192], P('kvp'), may hold values from 0.25 to 1.75
- gate_weight: bfloat16 [8192, 28672], P('kvp', 'tp'), may hold values from -0.0625 to 0.0625
- up_weight: bfloat16 [8192, 28672], P('kvp', 'tp'), may hold values from -0.0625 to 0.0625
- down_weight: bfloat16 [28672, 8192], P('tp', 'kvp'), may hold values from -0.03125 to 0.03125
Outputs:
- attended: bfloat16 [8, 8192], P(None, 'tp')
- layer_out: float32 [8, 8192], P(None, 'kvp')
Inputs may be any that keep to these rules, and one draw needn't show every extreme that they name: Row s is a permutation of 0 to 31; the page of request b's block j in KV shard s is s * 32 + block_table[s, b * 4 + j]. The lengths sum to 20480 and the longest is exactly 4096.
All inputs are finite; a program needn't handle non-finite values.
Results may differ from a plain program's by a relative error of at most 0.0056.
Values may be sent and summed in bfloat16 or wider, within the bound.
A program may use at most 128 MiB of HBM per device.

v0:
```python
import jax
import jax.numpy as jnp
from jax import lax
from jax.sharding import PartitionSpec as P

D = 8192
HD = 128


def merged(part, axis, combine):
    gathered = jax.tree.map(lambda a: lax.all_gather(a, axis), part)

    def take(source):
        return jax.tree.map(lambda a: lax.dynamic_index_in_dim(a, source, 0, False), gathered)

    return lax.fori_loop(
        1, lax.axis_size(axis), lambda source, state: combine(state, take(source)), take(0)
    )


def combine(earlier, later):
    peak_early, sum_early, out_early = earlier
    peak_late, sum_late, out_late = later
    row_peak = jnp.maximum(peak_early, peak_late)
    factor_early = jnp.exp(peak_early - row_peak)
    factor_late = jnp.exp(peak_late - row_peak)
    weight_sum = sum_early * factor_early + sum_late * factor_late
    out_sum = out_early * factor_early[..., None] + out_late * factor_late[..., None]
    return (row_peak, weight_sum, out_sum)


def body(
    queries,
    key_pool,
    value_pool,
    block_table,
    lengths,
    residual_in,
    out_weight,
    norm_gain,
    gate_weight,
    up_weight,
    down_weight,
):
    requests = queries.shape[0]
    kv_local = key_pool.shape[2] // HD
    heads_local = queries.shape[1] // HD
    group_size = heads_local // kv_local
    blocks = block_table.shape[1] // requests
    shard_span = blocks * key_pool.shape[1]
    shard_index = lax.axis_index("kvp")
    page_ids = block_table[0].reshape(requests, blocks)
    key_rows = key_pool[page_ids].reshape(requests, shard_span, kv_local, HD)
    value_rows = value_pool[page_ids].reshape(requests, shard_span, kv_local, HD)
    query_heads = queries.reshape(requests, kv_local, group_size, HD)
    scores = jnp.einsum(
        "bkgd,btkd->bkgt", query_heads, key_rows, preferred_element_type=jnp.float32
    ) * HD ** (-0.5)
    positions = shard_index * shard_span + jnp.arange(shard_span, dtype=jnp.int32)
    is_live = (positions[None, :] < lengths[:, None])[:, None, None, :]
    masked = jnp.where(is_live, scores, -1e30)
    row_peak = jnp.max(masked, axis=-1)
    weights = jnp.where(is_live, jnp.exp(masked - row_peak[..., None]), 0.0)
    weight_sum = jnp.sum(weights, axis=-1).reshape(requests, heads_local)
    rounded = weights.astype(jnp.bfloat16)
    out_sum = jnp.einsum("bkgt,btkd->bkgd", rounded, value_rows, preferred_element_type=jnp.float32)
    out_sum = out_sum.reshape(requests, heads_local, HD)
    row_peak = row_peak.reshape(requests, heads_local)
    row_peak, weight_sum, out_sum = merged((row_peak, weight_sum, out_sum), "kvp", combine)
    attended = (
        (out_sum / weight_sum[..., None]).astype(jnp.bfloat16).reshape(requests, heads_local * HD)
    )
    projected = jnp.dot(attended, out_weight, preferred_element_type=jnp.float32)
    mixed = residual_in + lax.psum(projected, "tp")
    squares = lax.psum(jnp.sum(mixed * mixed, axis=1), "kvp")
    inv_rms = lax.rsqrt(squares / D + 0.1)
    normed = (mixed * inv_rms[:, None] * norm_gain.astype(jnp.float32)).astype(jnp.bfloat16)
    gate_part = jnp.dot(normed, gate_weight, preferred_element_type=jnp.float32)
    up_part = jnp.dot(normed, up_weight, preferred_element_type=jnp.float32)
    gate_full, up_full = lax.psum((gate_part, up_part), "kvp")
    hidden = (jax.nn.silu(gate_full) * up_full).astype(jnp.bfloat16)
    down_part = jnp.dot(hidden, down_weight, preferred_element_type=jnp.float32)
    layer_out = mixed + lax.psum(down_part, "tp")
    return (attended, layer_out)


def solution(mesh):
    return jax.shard_map(
        body,
        mesh=mesh,
        in_specs=(
            P(None, "tp"),
            P("kvp", None, "tp"),
            P("kvp", None, "tp"),
            P("kvp", None),
            P(),
            P(None, "kvp"),
            P("tp", "kvp"),
            P("kvp"),
            P("kvp", "tp"),
            P("kvp", "tp"),
            P("tp", "kvp"),
        ),
        out_specs=(P(None, "tp"), P(None, "kvp")),
        check_vma=False,
    )
```

profile of v0, /device:TPU:0, one launch (start us, length us, event | category | flops | bytes accessed | tf_op | source)
XLA Modules:
  0.0 310.6 jit_solution(2432256013141088473)
XLA Ops:
  7.2 0.0 copy-start
  7.2 0.0 all-gather.2.cloned.1.call-start
  7.2 0.5 broadcast.76
  7.8 1.4 reduce.3
  9.1 0.1 reshape_squeeze.3
  9.2 0.1 reshape.83
  9.3 0.0 copy-done
  9.3 2.0 gather_fusion
  11.3 4.0 %reshape.77 = bf16[8,256,4,128]{3,2,1,0:T(4,128)(2,1)} reshape(bf16[32,64,512]{2,1,0:T(8,128)(2,1)} %gather_fusion) | data formatting | bytes 4194304 | tf_op jit(solution)/shard_map/reshape | solution.py:53
  15.3 3.6 %gather_fusion.1 = bf16[32,64,512]{2,1,0:T(8,128)(2,1)} fusion(bf16[32,64,512]{2,1,0:T(8,128)(2,1)} %param.15, s32[1024]{0:T(1024)S(1)} %pad_clamp_fusion), kind=kCustom, calls=%fused_computation.1 | custom fusion | bytes 4194432 | tf_op jit(solution)/shard_map/gather | solution.py:54
  18.9 0.0 copy-start.5
  18.9 0.0 copy-start.6
  18.9 4.0 %reshape.79 = bf16[8,256,4,128]{3,2,1,0:T(4,128)(2,1)} reshape(bf16[32,64,512]{2,1,0:T(8,128)(2,1)} %gather_fusion.1) | data formatting | bytes 4194304 | tf_op jit(solution)/shard_map/reshape | solution.py:54
  22.9 0.0 copy-done.5
  22.9 0.0 copy-start.1
  22.9 0.1 broadcast_compare_fusion
  22.9 0.0 copy-done.6
  23.0 2.5 fusion.34
  25.4 0.0 copy-start.4
  25.4 0.0 copy-done.1
  25.4 1.1 fusion.16
  26.5 0.0 all-gather.2.cloned.1.call-update
  26.6 0.0 all-reduce.3.cloned.1.call-start
  26.6 0.1 all_gather_reshape.9
  26.7 0.2 fusion.22
  26.9 0.1 all_gather_reshape.10
  27.0 0.0 copy-done.4
  27.0 42.8 %all_gather.10 = f32[16,8,32]{2,1,0:T(8,128)S(1)} all-gather(f32[1,8,32]{2,1,0:T(8,128)S(1)} %all_gather_reshape.10), channel_id=1, replica_groups=mesh['kvp'=16,'tp'=2] {'kvp'}, dimensions={0}, use_global_device_ids=true | all-gather | bytes 17408 | tf_op jit(solution)/shard_map/all_gather | solution.py:11
  69.8 36.0 %all_gather.9 = f32[16,8,32]{2,1,0:T(8,128)S(1)} all-gather(f32[1,8,32]{2,1,0:T(8,128)S(1)} %all_gather_reshape.9), channel_id=1, replica_groups=mesh['kvp'=16,'tp'=2] {'kvp'}, dimensions={0}, use_global_device_ids=true | all-gather | bytes 17408 | tf_op jit(solution)/shard_map/all_gather | solution.py:11
  105.9 0.0 all-gather.2.cloned.1.call-done
  105.9 0.9 slice_bitcast_fusion
  106.8 16.8 %while.19 = (s32[]{:T(128)}, f32[8,32]{1,0:T(8,128)S(1)}, f32[8,32]{1,0:T(8,128)S(1)}, f32[8,32,128]{2,1,0:T(8,128)S(1)}, f32[16,8,32]{2,1,0:T(8,128)S(1)}, /*in...) while((s32[]{:T(128)}, f32[8,32]{1,0:T(8,128)S(1)}, ...), condition=%wide.region_3.4_spmd, body=%wide.region_2.3_spmd.sunk | while | flops 99845 | bytes 403607 | solution.py:16
  106.8 1.1 fusion.44
  107.9 1.1 fusion.44
  109.1 1.1 fusion.44
  110.2 1.1 fusion.44
  111.3 1.1 fusion.44
  112.4 1.1 fusion.44
  113.5 1.1 fusion.44
  114.6 1.1 fusion.44
  115.8 1.1 fusion.44
  116.9 1.1 fusion.44
  118.0 1.1 fusion.44
  119.1 1.1 fusion.44
  120.2 1.1 fusion.44
  121.4 1.1 fusion.44
  122.5 1.1 fusion.44
  123.6 0.1 fusion.28
  123.7 0.0 copy-start.2
  123.7 0.0 copy-start.3
  123.7 2.9 fusion.35
  126.6 0.0 copy-done.2
  126.6 3.4 %psum.35 = f32[8,512]{1,0:T(8,128)S(1)} all-reduce(f32[8,512]{1,0:T(8,128)S(1)} %fusion.35), channel_id=1, replica_groups=mesh['kvp'=16,'tp'=2] {'tp'}, use_global_device_ids=true, to_apply=%region_4.5 | all-reduce | flops 4096 | bytes 32768 | tf_op jit(solution)/shard_map/psum | solution.py:74
  130.0 0.0 copy-done.3
  130.0 0.1 multiply_reduce_fusion
  130.1 38.6 %psum.36 = f32[8]{0:T(128)S(1)} all-reduce(f32[8]{0:T(128)S(1)} %get-tuple-element.201), channel_id=1, replica_groups=mesh['kvp'=16,'tp'=2] {'kvp'}, use_global_device_ids=true, to_apply=%region_6.7 | all-reduce | flops 8 | bytes 64 | tf_op jit(solution)/shard_map/psum | solution.py:75
  168.7 8.0 %fusion.32 = f32[8,14336]{1,0:T(8,128)} fusion(bf16[512,14336]{1,0:T(8,128)(2,1)} %param.21, f32[8,512]{1,0:T(8,128)S(1)} %get-tuple-element.202, f32[512]{0:T(512)S(1)} %convert_element_type.17, f32[8]{0:T(128)S(1)} %add_rsqrt_fusion), kind=kOutput, calls=%fused_computation.44 | convolution fusion | flops 117452800 | bytes 15157280 | tf_op jit(solution)/shard_map/dot_general | solution.py:78
  176.8 8.0 %fusion.31 = f32[8,14336]{1,0:T(8,128)} fusion(bf16[512,14336]{1,0:T(8,128)(2,1)} %param.22, f32[8,512]{1,0:T(8,128)S(1)} %get-tuple-element.202, f32[512]{0:T(512)S(1)} %convert_element_type.17, f32[8]{0:T(128)S(1)} %add_rsqrt_fusion), kind=kOutput, calls=%fused_computation.43 | convolution fusion | flops 117452800 | bytes 15157280 | tf_op jit(solution)/shard_map/dot_general | solution.py:79
  184.7 0.0 all-reduce.3.cloned.1.call-update
  184.8 107.5 %all-reduce.3.cloned.1.call-done = (f32[8,14336]{1,0:T(8,128)}, f32[8,14336]{1,0:T(8,128)}) async-done(((f32[8,14336]{1,0:T(8,128)}, f32[8,14336]{1,0:T(8,128)}), (f32[8,14336]{1,0:T(8,128)}, f32[8,14336]{1,0:T(8,128)})) %all-reduce.3.cloned.1.call-update) | async-done | bytes 917520 | tf_op jit(solution)/shard_map/psum | solution.py:80
  292.3 7.5 %fusion.19 = f32[8,512]{1,0:T(8,128)S(1)} fusion(bf16[14336,512]{1,0:T(8,128)(2,1)} %param.23, f32[8,14336]{1,0:T(8,128)} %get-tuple-element.195, f32[8,14336]{1,0:T(8,128)} %get-tuple-element.196), kind=kOutput, calls=%fused_computation.20 | convolution fusion | flops 118128640 | bytes 15613952 | tf_op jit(solution)/shard_map/dot_general | solution.py:82
  299.8 3.4 %psum.39 = f32[8,512]{1,0:T(8,128)S(1)} all-reduce(f32[8,512]{1,0:T(8,128)S(1)} %fusion.19), channel_id=1, replica_groups=mesh['kvp'=16,'tp'=2] {'tp'}, use_global_device_ids=true, to_apply=%region_9.10 | all-reduce | flops 4096 | bytes 32768 | tf_op jit(solution)/shard_map/psum | solution.py:83
  303.1 0.6 add.110
  (23 shorter events, 0.3 us)
Async XLA Ops:
  7.2 2.1 copy-start
  7.2 98.7 %all-gather.2.cloned.1.call-start = ((), (), s32[]{:S(2)}) async-start(), calls=%async_computation | async-start | bytes 2228224 | tf_op jit(solution)/shard_map/all_gather | solution.py:11
  18.9 4.0 %copy-start.5 = (s32[8]{0:T(128)S(1)}, s32[8]{0:T(128)}, u32[]{:S(2)}) copy-start(s32[8]{0:T(128)} %param.17) | copy-start | bytes 100
  18.9 4.1 %copy-start.6 = (bf16[8,4096]{1,0:T(8,128)(2,1)S(1)}, bf16[8,4096]{1,0:T(8,128)(2,1)}, u32[]{:S(2)}) copy-start(bf16[8,4096]{1,0:T(8,128)(2,1)} %param.13) | copy-start | bytes 196612
  22.9 2.5 copy-start.1
  25.4 1.6 copy-start.4
  26.6 265.7 %all-reduce.3.cloned.1.call-start = ((), (), s32[]{:S(2)}) async-start(), calls=%async_computation.1 | async-start | bytes 1835008 | tf_op jit(solution)/shard_map/psum | solution.py:80
  123.7 2.9 copy-start.2
  123.7 6.2 %copy-start.3 = (f32[8,512]{1,0:T(8,128)S(1)}, f32[8,512]{1,0:T(8,128)}, u32[]{:S(2)}) copy-start(f32[8,512]{1,0:T(8,128)} %param.18) | copy-start | bytes 49156
Sparse Core Ops, SparseCore 0:
  26.7 63.5 all-gather.1
  184.9 107.3 all-reduce.2
where the time goes:
time: 311 us
  blocking collectives  124 us (40%)
  waiting for transfers between devices  108 us (35%)
  matrix products  29.9 us (10%)
  other arithmetic  18.9 us (6%)
  local copies, waits for them, and re-layouts  15.4 us (5%)
  between operations  14.1 us (5%)
    psum x1, waiting for transfers between devices, body(): gate_full, up_full = lax.psum((gate_part, up_part), 'kvp')  108 us
    all_gather x2, blocking collectives, merged(): gathered = jax.tree.map(lambda a: lax.all_gather(a, axis), part)  78.9 us
    psum x1, blocking collectives, body(): squares = lax.psum(jnp.sum(mixed * mixed, axis=1), 'kvp')  38.6 us
    add x15, other arithmetic, combine(): out_early * factor_early[..., None] + out_late * factor_late[..., None]  16.1 us
    dot_general x1, matrix products, body(): gate_part = jnp.dot(normed, gate_weight, preferred_element_type=jnp.float32)  8.02 us
    dot_general x1, matrix products, body(): up_part = jnp.dot(normed, up_weight, preferred_element_type=jnp.float32)  7.99 us
    dot_general x1, matrix products, body(): down_part = jnp.dot(hidden, down_weight, preferred_element_type=jnp.float32)  7.46 us
  transfers between devices with their start and end apart: 2, of which 1 were waited for; matrix products, arithmetic and copies ran while one was open for 0% of the time, Pallas kernels for 0%

commit v1 on v0

--- a/solution.py
+++ b/solution.py
@@ -1,6 +1,9 @@
+import functools
 import jax
 import jax.numpy as jnp
 from jax import lax
+from jax.experimental import pallas as pl
+from jax.experimental.pallas import tpu as pltpu
 from jax.sharding import PartitionSpec as P
 
 D = 8192
@@ -29,7 +32,7 @@
     return (row_peak, weight_sum, out_sum)
 
 
-def body(
+def plain_body(
     queries,
     key_pool,
     value_pool,
@@ -84,6 +87,435 @@
     return (attended, layer_out)
 
 
+def remote(src, dst, send_sem, recv_sem, axis, target):
+    return pltpu.make_async_remote_copy(
+        src_ref=src,
+        dst_ref=dst,
+        send_sem=send_sem,
+        recv_sem=recv_sem,
+        device_id={axis: target},
+        device_id_type=pl.DeviceIdType.MESH,
+    )
+
+
+def layer_kernel(
+    sizes,
+    table,
+    lengths,
+    q_ref,
+    residual,
+    gain,
+    key_hbm,
+    value_hbm,
+    out_hbm,
+    gate_hbm,
+    up_hbm,
+    down_hbm,
+    attended,
+    layer_out,
+    keys,
+    values,
+    out_w,
+    gate_w,
+    up_w,
+    down_w,
+    o_send,
+    o_recv,
+    st_send,
+    st_recv,
+    att,
+    att_rows,
+    tp_buf,
+    sq,
+    gu_send,
+    gu_recv,
+    gu_own,
+    hid,
+    kv_sem,
+    w_sem,
+    gate_sem,
+    up_sem,
+    o_ss,
+    o_rs,
+    st_ss,
+    st_rs,
+    att_ss,
+    att_rs,
+    tp_ss,
+    tp_rs,
+    sq_ss,
+    sq_rs,
+    gu_ss,
+    gu_rs,
+    hid_ss,
+    hid_rs,
+):
+    n, t, requests, heads, kv_local, blocks, page, rp, chunk = sizes
+    me = lax.axis_index("kvp")
+    me_t = lax.axis_index("tp")
+    group = heads // kv_local
+    span = blocks * page
+    per_request = heads // rp
+    f32, bf16 = jnp.float32, jnp.bfloat16
+
+    def peer(i):
+        return lax.rem(me + i, n)
+
+    key_copy = pltpu.make_async_copy(key_hbm, keys, kv_sem.at[0])
+    value_copy = pltpu.make_async_copy(value_hbm, values, kv_sem.at[1])
+    key_copy.start()
+    value_copy.start()
+
+    barrier = pltpu.get_barrier_semaphore()
+    for i in range(1, n):
+        pl.semaphore_signal(
+            barrier, inc=1, device_id={"kvp": peer(i)}, device_id_type=pl.DeviceIdType.MESH
+        )
+    for i in range(1, t):
+        pl.semaphore_signal(
+            barrier,
+            inc=1,
+            device_id={"tp": lax.rem(me_t + i, t)},
+            device_id_type=pl.DeviceIdType.MESH,
+        )
+
+    def gate_copy(i):
+        columns = pl.ds(pl.multiple_of(peer(i + 1) * chunk, 128), chunk)
+        return pltpu.make_async_copy(gate_hbm.at[:, columns], gate_w.at[i], gate_sem.at[i])
+
+    def up_copy(i):
+        columns = pl.ds(pl.multiple_of(peer(i + 1) * chunk, 128), chunk)
+        return pltpu.make_async_copy(up_hbm.at[:, columns], up_w.at[i], up_sem.at[i])
+
+    out_copy = pltpu.make_async_copy(out_hbm, out_w, w_sem.at[0])
+    down_copy = pltpu.make_async_copy(down_hbm, down_w, w_sem.at[1])
+    key_copy.wait()
+    value_copy.wait()
+    out_copy.start()
+
+    @pl.loop(0, n)
+    def _(i):
+        gate_copy(i).start()
+        up_copy(i).start()
+
+    down_copy.start()
+    pl.semaphore_wait(barrier, n - 1 + t - 1)
+
+    row_h = lax.broadcasted_iota(jnp.int32, (heads, kv_local * HD), 0) // group
+    lane_k = lax.broadcasted_iota(jnp.int32, (heads, kv_local * HD), 1) // HD
+    on_block = row_h == lane_k
+    offsets = lax.broadcasted_iota(jnp.int32, (heads, span), 1)
+    lane = lax.broadcasted_iota(jnp.int32, (rp, HD), 1)
+    row = lax.broadcasted_iota(jnp.int32, (rp, HD), 0)
+    first = me // per_request
+
+    def o_copy(target, source):
+        return remote(
+            o_send.at[target], o_recv.at[source], o_ss.at[target], o_rs.at[source], "kvp", target
+        )
+
+    def st_copy(target, source):
+        return remote(
+            st_send.at[target], st_recv.at[source], st_ss.at[target], st_rs.at[source], "kvp", target
+        )
+
+    @pl.loop(0, requests)
+    def _(i):
+        b = lax.rem(first + i + 1, requests)
+        pages = [table[0, b * blocks + j] for j in range(blocks)]
+        key_rows = jnp.concatenate([keys[p] for p in pages], axis=0)
+        value_rows = jnp.concatenate([values[p] for p in pages], axis=0)
+        query = jnp.concatenate([q_ref[b]] * kv_local, axis=1)
+        query = jnp.where(on_block, query, 0.0).astype(bf16)
+        scores = lax.dot_general(
+            query, key_rows, (((1,), (1,)), ((), ())), preferred_element_type=f32
+        ) * HD ** (-0.5)
+        live = me * span + offsets < lengths[b]
+        masked = jnp.where(live, scores, -1e30)
+        peak = jnp.max(masked, axis=1, keepdims=True)
+        weights = jnp.where(live, jnp.exp(masked - peak), 0.0)
+        total = jnp.sum(weights, axis=1, keepdims=True)
+        wide = jnp.dot(weights.astype(bf16), value_rows, preferred_element_type=f32)
+        wide = jnp.where(on_block, wide, 0.0)
+        out = wide[:, :HD]
+        for k in range(1, kv_local):
+            out = out + wide[:, k * HD : (k + 1) * HD]
+        out = out.astype(bf16)
+        for c in range(per_request):
+            target = b * per_request + c
+            rows = slice(c * rp, (c + 1) * rp)
+            stats = jnp.where(lane == row, peak[rows], 0.0)
+            stats = jnp.where(lane == row + rp, total[rows], stats)
+            stats = jnp.sum(stats, axis=0, keepdims=True)
+
+            @pl.when(target == me)
+            def _():
+                o_recv[me] = out[rows]
+                st_recv[me] = stats
+
+            @pl.when(target != me)
+            def _():
+                o_send[target] = out[rows]
+                st_send[target] = stats
+                o_copy(target, me).start()
+                st_copy(target, me).start()
+
+    @pl.loop(1, n)
+    def _(i):
+        o_copy(me, peer(i)).wait_recv()
+        st_copy(me, peer(i)).wait_recv()
+
+    peaks, totals = [], []
+    for s in range(n):
+        stats = jnp.broadcast_to(st_recv[s], (rp, HD))
+        peaks.append(jnp.sum(jnp.where(lane == row, stats, 0.0), axis=1, keepdims=True))
+        totals.append(jnp.sum(jnp.where(lane == row + rp, stats, 0.0), axis=1, keepdims=True))
+    top = functools.reduce(jnp.maximum, peaks)
+    weight_sum = jnp.zeros((rp, 1), f32)
+    out_sum = jnp.zeros((rp, HD), f32)
+    for s in range(n):
+        factor = jnp.exp(peaks[s] - top)
+        weight_sum = weight_sum + totals[s] * factor
+        out_sum = out_sum + o_recv[s].astype(f32) * factor
+    att[me] = (out_sum / weight_sum).astype(bf16)
+
+    def att_copy(target, source):
+        return remote(
+            att.at[source], att.at[source], att_ss.at[target], att_rs.at[source], "kvp", target
+        )
+
+    @pl.loop(1, n)
+    def _(i):
+        att_copy(peer(i), me).start()
+
+    out_copy.wait()
+
+    @pl.loop(1, n)
+    def _(i):
+        att_copy(me, peer(i)).wait_recv()
+
+    for s in range(n):
+        att_rows[s * rp : (s + 1) * rp, :] = att[s].astype(f32)
+    whole = jnp.concatenate(
+        [att_rows[pl.ds(h, requests, stride=heads), :] for h in range(heads)], axis=1
+    ).astype(bf16)
+    attended[...] = whole
+
+    def over_tp(which, part):
+        def tp_copy(target, source):
+            return remote(
+                tp_buf.at[which, source],
+                tp_buf.at[which, source],
+                tp_ss.at[which, target],
+                tp_rs.at[which, source],
+                "tp",
+                target,
+            )
+
+        tp_buf[which, me_t] = part
+        for i in range(1, t):
+            tp_copy(lax.rem(me_t + i, t), me_t).start()
+        for i in range(1, t):
+            tp_copy(me_t, lax.rem(me_t + i, t)).wait_recv()
+        total = tp_buf[which, 0]
+        for s in range(1, t):
+            total = total + tp_buf[which, s]
+        for i in range(1, t):
+            tp_copy(lax.rem(me_t + i, t), me_t).wait_send()
+        return total
+
+    projected = jnp.dot(whole, out_w[...], preferred_element_type=f32)
+    mixed = residual[...] + over_tp(0, projected)
+
+    squares = jnp.sum(mixed * mixed, axis=1, keepdims=True)
+    sq[me] = jnp.broadcast_to(squares, (requests, HD))
+
+    def sq_copy(target, source):
+        return remote(
+            sq.at[source], sq.at[source], sq_ss.at[target], sq_rs.at[source], "kvp", target
+        )
+
+    @pl.loop(1, n)
+    def _(i):
+        sq_copy(peer(i), me).start()
+
+    scaled = (mixed * gain[...].astype(f32)).astype(bf16)
+    layer_out[...] = mixed
+
+    def gu_copy(target, source):
+        return remote(
+            gu_send.at[target], gu_recv.at[source], gu_ss.at[target], gu_rs.at[source], "kvp", target
+        )
+
+    def gate_up(i):
+        gate_copy(i).wait()
+        up_copy(i).wait()
+        gate = jnp.dot(scaled, gate_w[i], preferred_element_type=f32)
+        up = jnp.dot(scaled, up_w[i], preferred_element_type=f32)
+        return jnp.concatenate([gate, up], axis=0)
+
+    @pl.loop(0, n - 1)
+    def _(i):
+        target = peer(i + 1)
+        gu_send[target] = gate_up(i).astype(bf16)
+        gu_copy(target, me).start()
+
+    gu_own[...] = gate_up(n - 1)
+
+    @pl.loop(1, n)
+    def _(i):
+        sq_copy(me, peer(i)).wait_recv()
+
+    squares = sq[0]
+    for s in range(1, n):
+        squares = squares + sq[s]
+    inv_rms = lax.rsqrt(squares[:, :1] / (n * residual.shape[1]) + 0.1)
+
+    @pl.loop(1, n)
+    def _(i):
+        source = lax.rem(me + n - i, n)
+        gu_copy(me, source).wait_recv()
+        gu_own[...] += gu_recv[source].astype(f32)
+
+    gate = gu_own[:requests, :] * inv_rms
+    up = gu_own[requests:, :] * inv_rms
+    hid[me] = (gate / (1.0 + jnp.exp(-gate)) * up).astype(bf16)
+
+    def hid_copy(target, source):
+        return remote(
+            hid.at[source], hid.at[source], hid_ss.at[target], hid_rs.at[source], "kvp", target
+        )
+
+    @pl.loop(1, n)
+    def _(i):
+        hid_copy(peer(i), me).start()
+
+    down_copy.wait()
+
+    def down_step(i, acc):
+        source = lax.rem(me + n - i, n)
+        hid_copy(me, source).wait_recv()
+        return acc + jnp.dot(hid[source], down_w[source], preferred_element_type=f32)
+
+    acc = jnp.dot(hid[me], down_w[me], preferred_element_type=f32)
+    acc = lax.fori_loop(1, n, down_step, acc)
+    layer_out[...] = layer_out[...] + over_tp(1, acc)
+
+    @pl.loop(1, n)
+    def _(i):
+        target = peer(i)
+        o_copy(target, me).wait_send()
+        st_copy(target, me).wait_send()
+        att_copy(target, me).wait_send()
+        sq_copy(target, me).wait_send()
+        gu_copy(target, me).wait_send()
+        hid_copy(target, me).wait_send()
+
+
+def kernel_body(
+    queries,
+    key_pool,
+    value_pool,
+    block_table,
+    lengths,
+    residual_in,
+    out_weight,
+    norm_gain,
+    gate_weight,
+    up_weight,
+    down_weight,
+):
+    n, t = lax.axis_size("kvp"), lax.axis_size("tp")
+    requests = queries.shape[0]
+    heads = queries.shape[1] // HD
+    kv_local = key_pool.shape[2] // HD
+    blocks = block_table.shape[1] // requests
+    page = key_pool.shape[1]
+    rp = requests * heads // n
+    width, hidden = gate_weight.shape
+    chunk = hidden // n
+    sizes = (n, t, requests, heads, kv_local, blocks, page, rp, chunk)
+    f32, bf16 = jnp.float32, jnp.bfloat16
+    vmem = pl.BlockSpec(memory_space=pltpu.VMEM)
+    smem = pl.BlockSpec(memory_space=pltpu.SMEM)
+    hbm = pl.BlockSpec(memory_space=pl.ANY)
+    dma = pltpu.SemaphoreType.DMA
+    return pl.pallas_call(
+        functools.partial(layer_kernel, sizes),
+        out_shape=(
+            jax.ShapeDtypeStruct(queries.shape, bf16),
+            jax.ShapeDtypeStruct(residual_in.shape, f32),
+        ),
+        in_specs=[smem, smem, vmem, vmem, vmem, hbm, hbm, hbm, hbm, hbm, hbm],
+        out_specs=(vmem, vmem),
+        scratch_shapes=[
+            pltpu.VMEM(key_pool.shape, bf16),
+            pltpu.VMEM(value_pool.shape, bf16),
+            pltpu.VMEM(out_weight.shape, bf16),
+            pltpu.VMEM((n, width, chunk), bf16),
+            pltpu.VMEM((n, width, chunk), bf16),
+            pltpu.VMEM((n, chunk, width), bf16),
+            pltpu.VMEM((n, rp, HD), bf16),
+            pltpu.VMEM((n, rp, HD), bf16),
+            pltpu.VMEM((n, 1, HD), f32),
+            pltpu.VMEM((n, 1, HD), f32),
+            pltpu.VMEM((n, rp, HD), bf16),
+            pltpu.VMEM((n * rp, HD), f32),
+            pltpu.VMEM((2, t, requests, width), f32),
+            pltpu.VMEM((n, requests, HD), f32),
+            pltpu.VMEM((n, 2 * requests, chunk), bf16),
+            pltpu.VMEM((n, 2 * requests, chunk), bf16),
+            pltpu.VMEM((2 * requests, chunk), f32),
+            pltpu.VMEM((n, requests, chunk), bf16),
+            dma((2,)),
+            dma((2,)),
+            dma((n,)),
+            dma((n,)),
+            dma((n,)),
+            dma((n,)),
+            dma((n,)),
+            dma((n,)),
+            dma((n,)),
+            dma((n,)),
+            dma((2, t)),
+            dma((2, t)),
+            dma((n,)),
+            dma((n,)),
+            dma((n,)),
+            dma((n,)),
+            dma((n,)),
+            dma((n,)),
+        ],
+        compiler_params=pltpu.CompilerParams(
+            collective_id=0, has_side_effects=True, vmem_limit_bytes=60 * 1024 * 1024
+        ),
+    )(
+        block_table,
+        lengths,
+        queries.reshape(requests, heads, HD).astype(f32),
+        residual_in,
+        norm_gain.reshape(1, width),
+        key_pool,
+        value_pool,
+        out_weight,
+        gate_weight,
+        up_weight,
+        down_weight.reshape(n, chunk, width),
+    )
+
+
+def body(*arrays):
+    queries, gate_weight = arrays[0], arrays[8]
+    n = lax.axis_size("kvp")
+    requests = queries.shape[0]
+    heads = queries.shape[1] // HD
+    hidden = gate_weight.shape[1]
+    rp = requests * heads // n
+    tiled = rp % 16 == 0 and heads % rp == 0 and 2 * rp <= HD
+    tiled = tiled and requests * heads % n == 0 and hidden % (n * HD) == 0
+    return (kernel_body if tiled else plain_body)(*arrays)
+
+
 def solution(mesh):
     return jax.shard_map(
         body,

time: 311 us -> 58.7 us (0.19)
  blocking collectives: 124 us -> 0 us
  waiting for transfers between devices: 108 us -> 0 us
  Pallas kernels: 0 us -> 52.1 us
  matrix products: 29.9 us -> 0 us
  other arithmetic: 18.9 us -> 0.85 us
  between operations: 14.1 us -> 0.64 us
  local copies, waits for them, and re-layouts: 15.4 us -> 4.73 us
    psum x1 -> x0, waiting for transfers between devices: 108 us -> none  [body(): gate_full, up_full = lax.psum((gate_part, up_part), 'kvp')]
    all_gather x2 -> x0, blocking collectives: 78.9 us -> none  [merged(): gathered = jax.tree.map(lambda a: lax.all_gather(a, axis), part)]
    pallas_call x0 -> x1, Pallas kernels: none -> 52.1 us  [kernel_body(): pl.pallas_call(functools.partial(layer_kernel, sizes), out_shape=(jax.Sha...]
    psum x3 -> x0, blocking collectives: 45.4 us -> none  [the longest x1 38.6 us: body(): squares = lax.psum(jnp.sum(mixed * mixed, axis=1), 'kvp')]
    dot_general x6 -> x0, matrix products: 29.9 us -> none  [the longest x1 8.02 us: body(): gate_part = jnp.dot(normed, gate_weight, preferred_element_type=jnp.float32)]
    add x32 -> x0, other arithmetic: 17 us -> none  [the longest x15 16.1 us: combine(): out_early * factor_early[..., None] + out_late * factor_late[..., None]]
    reshape x2 -> x1, local copies, waits for them, and re-layouts: 7.98 us -> 1.26 us  [kernel_body(): norm_gain.reshape(1, width)]
    gather x2 -> x0, local copies, waits for them, and re-layouts: 5.57 us -> none  [the longest x1 3.6 us: body(): value_pool[page_ids].reshape(requests, shard_span, kv_local, HD)]
  transfers between devices with their start and end apart: 2 -> 0, of which waited for: 1 -> 0; matrix products, arithmetic and copies ran while one was open for 0% -> 0% of each run, Pallas kernels for 0% -> 0%
where the time goes in v1:
time: 58.7 us; the launch traced here: 58.4 us
  Pallas kernels  52.1 us (89%)
  local copies, waits for them, and re-layouts  4.73 us (8%)
  other arithmetic  0.85 us (1%)
  between operations  0.64 us (1%)
    pallas_call x1, Pallas kernels, kernel_body(): pl.pallas_call(functools.partial(layer_kernel, sizes), out_shape=(jax.Sha...  52.1 us
    unnamed x3, local copies, waits for them, and re-layouts  3.47 us
    reshape x1, local copies, waits for them, and re-layouts, kernel_body(): norm_gain.reshape(1, width)  1.26 us

profile of v1, /device:TPU:0, one launch (start us, length us, event | category | flops | bytes accessed | tf_op | source)
XLA Modules:
  0.0 58.4 jit_solution(85259631718343132)
XLA Ops:
  0.6 0.9 %convert_bitcast_fusion = f32[1,8,32,128]{3,1,2,0:T(8,128)S(1)} fusion(bf16[8,4096]{1,0:T(8,128)(2,1)} %param.11), kind=kLoop, calls=%fused_computation.1 | loop fusion | flops 32768 | bytes 196608
  1.5 0.7 %copy.15 = f32[1,8,32,128]{3,2,1,0:T(8,128)} copy(f32[1,8,32,128]{3,1,2,0:T(8,128)S(1)} %convert_bitcast_fusion) | data formatting | bytes 262144
  2.2 1.3 %reshape.13.gain = bf16[1,512]{1,0:T(2,128)(2,1)} reshape(bf16[512]{0:T(512)(128)(2,1)} %param.18) | data formatting | bytes 2048 | tf_op jit(solution)/shard_map/reshape | solution.py:497
  3.4 52.1 %shard_map.122 = (bf16[8,4096]{1,0:T(8,128)(2,1)}, f32[8,512]{1,0:T(8,128)}) custom-call(s32[1,32]{1,0:T(1,128)} %table.1, s32[8]{0:T(128)} %lengths.1, f32[8,32,128]{2,1,0:T(8,128)} %bitcast.7, f32[8,512]{1,0:T(8,128)} %residual.1, bf16[1,512]{1,0:T(2,128)(2,1)} %reshape.13.gain, bf16[32,64,512]{2,1,0:T(8,128)(2,1)} %key_hbm.1, ...), custom_call_target="tpu_custom_call" | custom-call | tf_op jit(solution)/shard_map/pallas_call | solution.py:443
  55.6 1.5 %copy.18 = bf16[8,4096]{1,0:T(8,128)(2,1)} copy(bf16[8,4096]{1,0:T(8,128)(2,1)} %get-tuple-element.4) | data formatting | bytes 131072
  57.0 1.3 %copy.19 = f32[8,512]{1,0:T(8,128)} copy(f32[8,512]{1,0:T(8,128)} %get-tuple-element.5) | data formatting | bytes 32768
